TPU v7x, 32 devices: a whole 2x2x4 slice. The times are simulated.
32 devices in a mesh: side: 8 (over y, x, core), lane: 4 (over z).
Axes of the slice: x: 2, y: 2, z: 4, core: 2. Of those that a mesh axis runs over, the one named last changes fastest.
Arguments:
- tokens: bfloat16 [4096, 2048], P(('side', 'lane')), may hold values from -6 to 6
- expert_ids: int32 [4096, 8], P(('side', 'lane')), may hold values from 0 to 31, all different within a row; in each aligned block of 128 rows (0 to 127, 128 to 255, ...) at most 64 rows name the same one
- route_weights: float32 [4096, 8], P(('side', 'lane')), may hold values from 0.03 to 0.4
- w_gate: bfloat16 [32, 2048, 768], P(('side', 'lane')), may hold values from -0.125 to 0.125
- w_up: bfloat16 [32, 2048, 768], P(('side', 'lane')), may hold values from -0.125 to 0.125
- w_down: bfloat16 [32, 768, 2048], P(('side', 'lane')), may hold values from -0.21875 to 0.21875
Outputs:
- mixed: bfloat16 [4096, 2048], P(('side', 'lane'))
Inputs may be any that keep to these rules, and one draw needn't show every extreme that they name: `expert_ids`: each row names 8 different experts. Within each aligned block of 128 rows (the rows of one device) no expert is named by more than 64 rows, and in every draw some expert is named by exactly 64 rows of some block.
All inputs are finite; a program needn't handle non-finite values.
Results may differ from a plain program's by a relative error of at most 0.0085.
Values may be sent and summed in bfloat16 or wider, within the bound.
A program may use at most 128 MiB of HBM per device.

v0:
```python
import jax
import jax.numpy as jnp
from jax import lax
from jax.sharding import PartitionSpec as P


def expert_ffn(rows, gate_proj, up_proj, down_proj):
    gate = jnp.dot(rows, gate_proj, preferred_element_type=jnp.float32)
    upper = jnp.dot(rows, up_proj, preferred_element_type=jnp.float32)
    hidden = (jax.nn.silu(gate) * upper).astype(jnp.bfloat16)
    return jnp.dot(hidden, down_proj, preferred_element_type=jnp.float32).astype(jnp.bfloat16)


def on_device(tokens, expert_ids, route_weights, w_gate, w_up, w_down):
    tok_rows = tokens.shape[0]
    width = tokens.shape[1]
    top_count = expert_ids.shape[1]
    side_count = lax.axis_size("side")
    device_count = side_count * lax.axis_size("lane")
    local_count = w_gate.shape[0]
    expert_count = device_count * local_count
    capacity = 2 * tok_rows * top_count // expert_count
    flat_ids = expert_ids.reshape(-1)
    onehot = (flat_ids[:, None] == jnp.arange(expert_count, dtype=jnp.int32)[None, :]).astype(
        jnp.int32
    )
    earlier = jnp.cumsum(onehot, axis=0) - onehot
    slot_index = jnp.sum(earlier * onehot, axis=1)
    position = (flat_ids * capacity + slot_index).reshape(tok_rows, top_count)
    buffer_rows = jnp.arange(expert_count * capacity, dtype=jnp.int32)
    dispatch_table = jnp.any(buffer_rows[:, None, None] == position[None, :, :], axis=2).astype(
        jnp.bfloat16
    )
    outgoing = jnp.dot(dispatch_table, tokens, preferred_element_type=jnp.float32).astype(
        jnp.bfloat16
    )
    outgoing = outgoing.reshape(expert_count, capacity, width)
    received = lax.all_to_all(outgoing, ("side", "lane"), split_axis=0, concat_axis=0, tiled=True)
    count = received.shape[1]
    grouped = received.reshape(device_count, local_count, count, width)
    rows = grouped[:, 0].reshape(device_count * count, width)
    output = expert_ffn(rows, w_gate[0], w_up[0], w_down[0])
    results = [output.reshape(device_count, count, width)]
    returned = lax.all_to_all(
        jnp.stack(results, axis=1).reshape(device_count * local_count, count, width),
        ("side", "lane"),
        split_axis=0,
        concat_axis=0,
        tiled=True,
    )
    flat_back = returned.reshape(expert_count * capacity, width)
    picked = flat_back[position]
    mixed = jnp.einsum("tk,tkd->td", route_weights, picked, preferred_element_type=jnp.float32)
    return mixed.astype(jnp.bfloat16)


def solution(mesh):
    placed = (
        P(("side", "lane"), None),
        P(("side", "lane"), None),
        P(("side", "lane"), None),
        P(("side", "lane"), None, None),
        P(("side", "lane"), None, None),
        P(("side", "lane"), None, None),
    )
    return jax.shard_map(
        on_device, mesh=mesh, in_specs=placed, out_specs=P(("side", "lane"), None), check_vma=False
    )
```

profile of v0, /device:TPU:0, one launch (start us, length us, event | category | flops | bytes accessed | tf_op | source)
XLA Modules:
  0.0 448.5 jit_solution(18093856621233300722)
XLA Ops:
  0.0 0.0 copy-start
  0.0 0.9 copy.21
  0.9 0.1 eq.43
  1.0 0.1 eq.39
  1.1 9.0 %reduce-window.6 = s32[32,8,128]{2,1,0:T(8,128)S(1)} reduce-window(s32[32,8,128]{2,1,0:T(8,128)S(1)} %fusion.12, s32[]{:T(128)} %constant.4.clone.1), window={size=1x1x128 pad=0_0x0_0x127_0}, to_apply=%region_0.0 | reduce-window | flops 4161536 | bytes 262148 | tf_op jit(solution)/shard_map/reduce-window
  10.2 0.1 slice.10
  10.3 0.1 copy.23
  10.4 0.1 copy.24
  10.5 0.1 broadcast_add_fusion
  10.7 0.1 reduce_sum.12
  10.8 0.7 compare_select_fusion
  11.5 7.4 %fusion = pred[2048,128]{1,0:T(8,128)(4,1)S(1)} fusion(s32[128,8]{0,1:T(8,128)S(1)} %get-tuple-element.6), kind=kLoop, calls=%fused_computation.2 | loop fusion | flops 3932160 | bytes 266240 | tf_op jit(solution)/shard_map/reduce_or | solution.py:31
  18.9 3.4 convolution_convert_fusion.1
  22.3 0.0 copy-start.3
  22.3 189.4 %all_to_all.10 = bf16[32,64,2048]{2,1,0:T(8,128)(2,1)S(1)} all-to-all(bf16[32,64,2048]{2,1,0:T(8,128)(2,1)S(1)} %bitcast.44), channel_id=1, replica_groups=mesh['side'=8,'lane'=4] {'side','lane'}, dimensions={0} | all-to-all | bytes 16777216 | tf_op jit(solution)/shard_map/all_to_all | solution.py:38
  211.7 0.0 copy-start.1
  211.7 3.2 copy-done.1
  214.9 0.0 copy-done.3
  214.9 8.6 %fusion.6 = f32[2048,768]{1,0:T(8,128)} fusion(bf16[2048,2048]{1,0:T(8,128)(2,1)S(1)} %bitcast.46, bf16[1,2048,768]{2,1,0:T(8,128)(2,1)S(1)} %copy-done.3), kind=kOutput, calls=%fused_computation.10 | convolution fusion | flops 6442450944 | bytes 17825792 | tf_op jit(solution)/shard_map/dot_general | solution.py:8
  223.4 0.0 copy-done
  223.4 21.3 %convolution_convert_fusion = bf16[2048,2048]{1,0:T(8,128)(2,1)} fusion(f32[2048,768]{1,0:T(8,128)} %fusion.6, bf16[2048,2048]{1,0:T(8,128)(2,1)} %bitcast.47, bf16[1,768,2048]{2,1,0:T(8,128)(2,1)S(1)} %copy-done, bf16[1,2048,768]{2,1,0:T(8,128)(2,1)} %param.10), kind=kOutput, calls=%fused_computation.3 | convolution fusion | flops 12898533376 | bytes 29360128 | tf_op jit(solution)/shard_map/dot_general | solution.py:11
  244.7 0.0 copy-start.2
  244.7 4.7 %all-to-all-start.1 = ((bf16[32,64,2048]{2,1,0:T(8,128)(2,1)}), bf16[32,64,2048]{2,1,0:T(8,128)(2,1)}, u32[]{:S(2)}, u32[]{:S(2)}) async-start(bf16[32,64,2048]{2,1,0:T(8,128)(2,1)} %bitcast.45), calls=%async_computation.1 | async-start | bytes 16777216 | tf_op jit(solution)/shard_map/all_to_all | solution.py:44
  249.4 0.1 copy.26
  249.5 0.1 reshape.37
  249.6 0.0 copy-done.2
  249.6 0.1 copy.27
  249.8 181.0 %all-to-all-done.1 = bf16[32,64,2048]{2,1,0:T(8,128)(2,1)} async-done(((bf16[32,64,2048]{2,1,0:T(8,128)(2,1)}), bf16[32,64,2048]{2,1,0:T(8,128)(2,1)}, u32[]{:S(2)}, u32[]{:S(2)}) %all-to-all-start.1) | async-done | bytes 8388640 | tf_op jit(solution)/shard_map/all_to_all | solution.py:44
  430.7 13.3 %gather_fusion = bf16[1024,2048]{1,0:T(8,128)(2,1)} fusion(bf16[2048,2048]{1,0:T(8,128)(2,1)} %bitcast.8, s32[1024]{0:T(1024)S(1)} %broadcast_clamp_fusion), kind=kCustom, calls=%fused_computation | custom fusion | bytes 8392704 | tf_op jit(solution)/shard_map/gather | solution.py:52
  444.0 3.4 fusion.1
  447.4 1.1 copy.32
  (6 shorter events, 0.1 us)
Async XLA Ops:
  0.0 223.4 %copy-start = (bf16[1,768,2048]{2,1,0:T(8,128)(2,1)S(1)}, bf16[1,768,2048]{2,1,0:T(8,128)(2,1)}, u32[]{:S(2)}) copy-start(bf16[1,768,2048]{2,1,0:T(8,128)(2,1)} %param.11) | copy-start | bytes 9437188
  22.3 192.6 %copy-start.3 = (bf16[1,2048,768]{2,1,0:T(8,128)(2,1)S(1)}, bf16[1,2048,768]{2,1,0:T(8,128)(2,1)}, u32[]{:S(2)}) copy-start(bf16[1,2048,768]{2,1,0:T(8,128)(2,1)} %param.9) | copy-start | bytes 9437188
  211.7 3.2 copy-start.1
  244.7 4.9 %copy-start.2 = (f32[128,8]{0,1:T(8,128)S(1)}, f32[128,8]{0,1:T(8,128)}, u32[]{:S(2)}) copy-start(f32[128,8]{0,1:T(8,128)} %param.8) | copy-start | bytes 12292
  244.7 186.0 %all-to-all-start.1 = ((bf16[32,64,2048]{2,1,0:T(8,128)(2,1)}), bf16[32,64,2048]{2,1,0:T(8,128)(2,1)}, u32[]{:S(2)}, u32[]{:S(2)}) async-start(bf16[32,64,2048]{2,1,0:T(8,128)(2,1)} %bitcast.45), calls=%async_computation.1 | async-start | bytes 16777216 | tf_op jit(solution)/shard_map/all_to_all | solution.py:44
where the time goes:
time: 453 us; the launch traced here: 449 us
  blocking collectives  189 us (42%)
  waiting for transfers between devices  181 us (40%)
  matrix products  36.6 us (8%)
  local copies, waits for them, and re-layouts  19.5 us (4%)
  other arithmetic  17.3 us (4%)
  starting transfers between devices  4.68 us (1%)
    all_to_all x1, blocking collectives, on_device(): lax.all_to_all(outgoing, ('side', 'lane'), split_axis=0, concat_axis=0, t...  189 us
    all_to_all x1, waiting for transfers between devices, on_device(): lax.all_to_all(jnp.stack(results, axis=1).reshape(device_count * local_co...  181 us
    dot_general x1, matrix products, expert_ffn(): jnp.dot(hidden, down_proj, preferred_element_type=jnp.float32)  21.3 us
    gather x1, local copies, waits for them, and re-layouts, on_device(): picked = flat_back[position]  13.3 us
    another operation x3, other arithmetic  9.15 us
  transfers between devices with their start and end apart: 1, of which 1 were waited for; matrix products, arithmetic and copies ran while one was open for 0% of the time, Pallas kernels for 0%

commit v1 on v0

v1 whole, which is shorter than its diff:
```python
import jax
import jax.numpy as jnp
from jax import lax
from jax.sharding import PartitionSpec as P

AXES = ("side", "lane")


def on_device(tokens, expert_ids, route_weights, w_gate, w_up, w_down):
    tok_rows, width = tokens.shape
    top_count = expert_ids.shape[1]
    device_count = lax.axis_size("side") * lax.axis_size("lane")
    capacity = 2 * tok_rows * top_count // device_count
    experts = jnp.arange(device_count, dtype=jnp.int32)
    weight = jnp.sum(
        jnp.where(expert_ids[:, :, None] == experts[None, None, :], route_weights[:, :, None], 0.0),
        axis=1,
    )
    me = lax.axis_index("side") * lax.axis_size("lane") + lax.axis_index("lane")
    every = lax.all_gather(tokens, AXES, axis=0, tiled=True).reshape(device_count, tok_rows, width)
    weights = lax.all_to_all(weight.T, AXES, split_axis=0, concat_axis=0, tiled=True)
    chosen = weights > 0.0
    counted = chosen.astype(jnp.int32)
    slot = jnp.cumsum(counted, axis=1) - counted
    table = (slot[:, None, :] == jnp.arange(capacity, dtype=jnp.int32)[None, :, None]) & chosen[
        :, None, :
    ]
    pick = table.astype(jnp.bfloat16)
    rows = jnp.einsum("bst,btd->bsd", pick, every, preferred_element_type=jnp.float32).astype(
        jnp.bfloat16
    )
    rows = rows.reshape(device_count * capacity, width)
    gate = jnp.dot(rows, w_gate[0], preferred_element_type=jnp.float32)
    upper = jnp.dot(rows, w_up[0], preferred_element_type=jnp.float32)
    hidden = (jax.nn.silu(gate) * upper).astype(jnp.bfloat16)
    output = jnp.dot(hidden, w_down[0], preferred_element_type=jnp.float32).astype(jnp.bfloat16)
    output = output.reshape(device_count, capacity, width)
    back = (pick.astype(jnp.float32) * weights[:, None, :]).astype(jnp.bfloat16)
    part = jnp.einsum("bst,bsd->btd", back, output, preferred_element_type=jnp.float32).astype(
        jnp.bfloat16
    )
    part = part.reshape(device_count * tok_rows, width)
    return lax.psum_scatter(part, AXES, scatter_dimension=0, tiled=True)


def solution(mesh):
    placed = (
        P(AXES, None),
        P(AXES, None),
        P(AXES, None),
        P(AXES, None, None),
        P(AXES, None, None),
        P(AXES, None, None),
    )
    return jax.shard_map(
        on_device, mesh=mesh, in_specs=placed, out_specs=P(AXES, None), check_vma=False
    )
```

time: 453 us -> 551 us (1.22)
  waiting for transfers between devices: 181 us -> 464 us
  blocking collectives: 189 us -> 14.3 us
  matrix products: 36.6 us -> 57.1 us
  local copies, waits for them, and re-layouts: 19.5 us -> 0.01 us
  other arithmetic: 17.3 us -> 1.2 us
  between operations: 0.12 us -> 13.4 us
    reduce_scatter x0 -> x1, waiting for transfers between devices: none -> 359 us  [on_device(): return lax.psum_scatter(part, AXES, scatter_dimension=0, tiled=True)]
    all_to_all x1 -> x0, waiting for transfers between devices: 181 us -> none  [on_device(): lax.all_to_all(jnp.stack(results, axis=1).reshape(device_count * local_co...]
    all_to_all x1, blocking collectives: 189 us -> 14.3 us  [on_device(): lax.all_to_all(weight.T, AXES, split_axis=0, concat_axis=0, tiled=True)]
    all_gather x0 -> x1, waiting for transfers between devices: none -> 105 us  [on_device(): lax.all_gather(tokens, AXES, axis=0, tiled=True)]
    dot_general x4, matrix products: 36.6 us -> 57.1 us  [the longest x1 21.3 us: on_device(): jnp.dot(hidden, w_down[0], preferred_element_type=jnp.float32)]
    gather x1 -> x0, local copies, waits for them, and re-layouts: 13.3 us -> none  [on_device(): picked = flat_back[position]]
    another operation x3 -> x1, other arithmetic: 9.15 us -> 0.28 us  [on_device(): slot = jnp.cumsum(counted, axis=1) - counted]
    reduce_or x1 -> x0, other arithmetic: 7.41 us -> none  [on_device(): jnp.any(buffer_rows[:, None, None] == position[None, :, :], axis=2)]
  transfers between devices with their start and end apart: 1 -> 2, of which waited for: 1 -> 2; matrix products, arithmetic and copies ran while one was open for 0% -> 0% of each run, Pallas kernels for 0% -> 0%
where the time goes in v1:
time: 551 us; the launch traced here: 550 us
  waiting for transfers between devices  464 us (84%)
  matrix products  57.1 us (10%)
  blocking collectives  14.3 us (3%)
  between operations  13.4 us (2%)
    reduce_scatter x1, waiting for transfers between devices, on_device(): return lax.psum_scatter(part, AXES, scatter_dimension=0, tiled=True)  359 us
    all_gather x1, waiting for transfers between devices, on_device(): lax.all_gather(tokens, AXES, axis=0, tiled=True)  105 us
    dot_general x1, matrix products, on_device(): jnp.dot(hidden, w_down[0], preferred_element_type=jnp.float32)  21.3 us
    all_to_all x1, blocking collectives, on_device(): lax.all_to_all(weight.T, AXES, split_axis=0, concat_axis=0, tiled=True)  14.3 us
    dot_general x1, matrix products, on_device(): jnp.einsum('bst,bsd->btd', back, output, preferred_element_type=jnp.float32)  13.6 us
    dot_general x1, matrix products, on_device(): jnp.einsum('bst,btd->bsd', pick, every, preferred_element_type=jnp.float32)  11.5 us
  transfers between devices with their start and end apart: 2, of which 2 were waited for; matrix products, arithmetic and copies ran while one was open for 0% of the time, Pallas kernels for 0%

profile of v1, /device:TPU:0, one launch (start us, length us, event | category | flops | bytes accessed | tf_op | source)
XLA Modules:
  0.0 550.4 jit_solution(13425072589977639435)
XLA Ops:
  6.5 0.0 copy-start
  6.5 0.0 all-gather.2.cloned.1.call-start
  6.5 0.7 all-gather.2.cloned.1.call-update
  7.3 0.0 reduce-scatter.2.cloned.1.call-start
  7.3 0.9 select_reduce_fusion
  8.2 14.3 %all_to_all.12 = f32[32,1,128]{2,1,0:T(1,128)S(1)} all-to-all(f32[32,1,128]{2,1,0:T(1,128)S(1)} %bitcast.37), channel_id=1, replica_groups=mesh['side'=8,'lane'=4] {'side','lane'}, dimensions={0} | all-to-all | bytes 32768 | tf_op jit(solution)/shard_map/all_to_all | solution.py:21
  22.5 0.3 reduce_window_sum.11
  22.8 104.6 %all-gather.2.cloned.1.call-done = bf16[4096,2048]{1,0:T(8,128)(2,1)} async-done(((bf16[128,2048]{1,0:T(8,128)(2,1)}), bf16[4096,2048]{1,0:T(8,128)(2,1)}) %all-gather.2.cloned.1.call-update) | async-done | bytes 16777232 | tf_op jit(solution)/shard_map/all_gather | solution.py:20
  127.4 0.0 copy-start.2
  127.4 11.5 %convolution_convert_fusion.2 = bf16[32,64,2048]{2,1,0:T(8,128)(2,1)} fusion(bf16[32,128,2048]{2,1,0:T(8,128)(2,1)} %bitcast.29, s32[32,128]{1,0:T(8,128)S(1)} %subtract_bitcast_fusion, pred[32,128]{1,0:T(8,128)(4,1)S(1)} %bitcast.35), kind=kOutput, calls=%fused_computation.3 | convolution fusion | flops 1078460416 | bytes 25186304 | tf_op jit(solution)/shard_map/bst,btd->bsd/dot_general | solution.py:29
  138.9 0.0 copy-done.2
  138.9 10.7 %fusion.3 = f32[2048,768]{1,0:T(8,128)} fusion(bf16[2048,2048]{1,0:T(8,128)(2,1)} %bitcast.31, bf16[1,2048,768]{2,1,0:T(8,128)(2,1)S(1)} %copy-done.2), kind=kOutput, calls=%fused_computation.6 | convolution fusion | flops 6442450944 | bytes 17825792 | tf_op jit(solution)/shard_map/dot_general | solution.py:33
  149.6 0.0 copy-done
  149.6 21.3 %convolution_convert_fusion.1 = bf16[2048,2048]{1,0:T(8,128)(2,1)} fusion(f32[2048,768]{1,0:T(8,128)} %fusion.3, bf16[2048,2048]{1,0:T(8,128)(2,1)} %bitcast.32, bf16[1,768,2048]{2,1,0:T(8,128)(2,1)S(1)} %copy-done, bf16[1,2048,768]{2,1,0:T(8,128)(2,1)} %param.10), kind=kOutput, calls=%fused_computation.1 | convolution fusion | flops 12898533376 | bytes 29360128 | tf_op jit(solution)/shard_map/dot_general | solution.py:36
  170.9 13.6 %convolution_convert_fusion = bf16[32,128,2048]{2,1,0:T(8,128)(2,1)} fusion(bf16[32,64,2048]{2,1,0:T(8,128)(2,1)} %bitcast.30, f32[32,128]{1,0:T(8,128)S(1)} %bitcast.34, s32[32,128]{1,0:T(8,128)S(1)} %subtract_bitcast_fusion, pred[32,128]{1,0:T(8,128)(4,1)S(1)} %bitcast.36), kind=kOutput, calls=%fused_computation | convolution fusion | flops 1083703296 | bytes 25202688 | tf_op jit(solution)/shard_map/bst,bsd->btd/dot_general | solution.py:39
  184.5 0.0 copy-start.1
  184.5 0.0 reduce-scatter.2.cloned.1.call-update
  184.6 359.0 %reduce-scatter.2.cloned.1.call-done = bf16[128,2048]{1,0:T(8,128)(2,1)} async-done(((bf16[4096,2048]{1,0:T(8,128)(2,1)}), bf16[128,2048]{1,0:T(8,128)(2,1)}) %reduce-scatter.2.cloned.1.call-update) | async-done | bytes 524304 | tf_op jit(solution)/shard_map/reduce_scatter | solution.py:43
  543.6 0.0 copy-done.1
  (2 shorter events, 0.0 us)
Async XLA Ops:
  6.5 143.1 %copy-start = (bf16[1,768,2048]{2,1,0:T(8,128)(2,1)S(1)}, bf16[1,768,2048]{2,1,0:T(8,128)(2,1)}, u32[]{:S(2)}) copy-start(bf16[1,768,2048]{2,1,0:T(8,128)(2,1)} %param.11) | copy-start | bytes 9437188
  6.5 120.9 %all-gather.2.cloned.1.call-start = ((), (), s32[]{:S(2)}) async-start(), calls=%async_computation.2 | async-start | bytes 17301504 | tf_op jit(solution)/shard_map/all_gather | solution.py:20
  7.3 536.3 %reduce-scatter.2.cloned.1.call-start = ((), (), s32[]{:S(2)}) async-start(), calls=%async_computation.3 | async-start | bytes 17301504 | tf_op jit(solution)/shard_map/reduce_scatter | solution.py:43
  127.4 11.5 %copy-start.2 = (bf16[1,2048,768]{2,1,0:T(8,128)(2,1)S(1)}, bf16[1,2048,768]{2,1,0:T(8,128)(2,1)}, u32[]{:S(2)}) copy-start(bf16[1,2048,768]{2,1,0:T(8,128)(2,1)} %param.9) | copy-start | bytes 9437188
  184.5 359.0 %copy-start.1 = (bf16[1,768,2048]{2,1,0:T(8,128)(2,1)S(1)}, bf16[1,768,2048]{2,1,0:T(8,128)(2,1)}, u32[]{:S(2)}) copy-start(bf16[1,768,2048]{2,1,0:T(8,128)(2,1)} %param.11) | copy-start | bytes 9437188
Sparse Core Ops, SparseCore 0:
  10.3 117.0 all-gather.1
  184.7 358.8 reduce-scatter.1

commit v2 on v0

--- a/solution.py
+++ b/solution.py
@@ -1,7 +1,287 @@
+import functools
+
 import jax
 import jax.numpy as jnp
 from jax import lax
+from jax.experimental import pallas as pl
+from jax.experimental.pallas import tpu as pltpu
 from jax.sharding import PartitionSpec as P
+
+AXES = ("side", "lane")
+MESH = pl.DeviceIdType.MESH
+BF16 = jnp.bfloat16
+F32 = jnp.float32
+
+
+def flip(value, mask):
+    bit = 1
+    out = value
+    while bit <= mask:
+        if mask & bit:
+            out = out + bit - 2 * bit * ((value // bit) % 2)
+        bit *= 2
+    return out
+
+
+def place(levels):
+    side = lax.axis_index("side")
+    level = lax.axis_index("lane")
+    return side // 2, side % 2, level
+
+
+def greet(devices):
+    barrier = pltpu.get_barrier_semaphore()
+    for device in devices:
+        pl.semaphore_signal(barrier, inc=1, device_id=device, device_id_type=MESH)
+    pl.semaphore_wait(barrier, len(devices))
+
+
+def gather_kernel(
+    levels, tokens, mine, wg, wu, wd, every, shares, wg2, wu2, wd2, send, recv, ssend, srecv, wsend, wrecv, local
+):
+    col, core, level = place(levels)
+    half = tokens.shape[0] // 2
+    chips = every.shape[0]
+    col_x, col_y = flip(col, 1), flip(col, 2)
+    dev_x, dev_y = (col_x * 2 + core, level), (col_y * 2 + core, level)
+    twin = (col * 2 + 1 - core, level)
+    me = col * levels + level
+    others = [
+        (flip(col, m // levels), flip(level, m % levels)) for m in range(1, chips)
+    ]
+    greet([(q * 2 + core, z) for q, z in others] + [twin])
+
+    started = []
+
+    def go(src, dst, s, r, device):
+        copy = pltpu.make_async_remote_copy(
+            src_ref=src, dst_ref=dst, send_sem=s, recv_sem=r, device_id=device, device_id_type=MESH
+        )
+        copy.start()
+        started.append(copy)
+        return copy
+
+    for i, (q, z) in enumerate(others):
+        go(mine.at[q * levels + z], shares.at[me], ssend.at[i], srecv.at[i], (q * 2 + core, z))
+    keep = [
+        pltpu.make_async_copy(tokens, every.at[me], local.at[0]),
+        pltpu.make_async_copy(mine.at[me], shares.at[me], local.at[1]),
+    ]
+    for copy in keep:
+        copy.start()
+
+    lanes = []
+    top, low = pl.ds(0, half), pl.ds(half, half)
+    waited = set()
+    for k in range(levels):
+        z = flip(level, k)
+        b = col * levels + z
+        if k:
+            lanes[k - 1].wait_recv()
+            waited.add(id(lanes[k - 1]))
+            block = every.at[b]
+        else:
+            block = tokens
+        a = go(block.at[top], every.at[b, top], send.at[1, k], recv.at[1, k], dev_x)
+        c = go(block.at[low], every.at[b, low], send.at[2, k], recv.at[2, k], dev_y)
+        if k == 0:
+            for m in range(1, levels):
+                lanes.append(
+                    go(tokens, every.at[me], send.at[0, m], recv.at[0, m], (col * 2 + core, flip(level, m)))
+                )
+        go(block.at[low], every.at[b, low], send.at[3, k], recv.at[3, k], dev_x)
+        go(block.at[top], every.at[b, top], send.at[4, k], recv.at[4, k], dev_y)
+        if k == 0:
+            go(wg, wg2, wsend.at[0], wrecv.at[0], twin)
+            go(wu, wu2, wsend.at[1], wrecv.at[1], twin)
+            go(wd, wd2, wsend.at[2], wrecv.at[2], twin)
+        a.wait_recv()
+        waited.add(id(a))
+        bx = every.at[col_x * levels + z, top]
+        go(bx, bx, send.at[5, k], recv.at[5, k], dev_y)
+        c.wait_recv()
+        waited.add(id(c))
+        by = every.at[col_y * levels + z, low]
+        go(by, by, send.at[6, k], recv.at[6, k], dev_x)
+    for copy in started:
+        if id(copy) not in waited:
+            copy.wait_recv()
+        copy.wait_send()
+    for copy in keep:
+        copy.wait()
+
+
+def return_kernel(levels, part, out, first, second, third, fold, level_sum, send, recv):
+    col, core, level = place(levels)
+    rows = out.shape[0]
+    half = rows // 2
+    col_x, col_y, col_xy = flip(col, 1), flip(col, 2), flip(flip(col, 1), 2)
+    dev_x, dev_y = (col_x * 2 + core, level), (col_y * 2 + core, level)
+    greet([dev_x, dev_y] + [(col * 2 + core, flip(level, m)) for m in range(1, levels)])
+    top, low = pl.ds(0, half), pl.ds(half, half)
+    started = []
+
+    def go(src, dst, i, k, device):
+        copy = pltpu.make_async_remote_copy(
+            src_ref=src,
+            dst_ref=dst,
+            send_sem=send.at[i, k],
+            recv_sem=recv.at[i, k],
+            device_id=device,
+            device_id_type=MESH,
+        )
+        copy.start()
+        started.append(copy)
+        return copy
+
+    def add(dst, one, two):
+        dst[...] = (one[...].astype(F32) + two[...].astype(F32)).astype(BF16)
+
+    def stage_one(k):
+        z = flip(level, k)
+        return [
+            go(part.at[col_xy * levels + z, top], first.at[k, 0, 0], 0, k, dev_x),
+            go(part.at[col_xy * levels + z, low], first.at[k, 1, 0], 1, k, dev_y),
+            go(part.at[col_x * levels + z, top], first.at[k, 0, 1], 2, k, dev_x),
+            go(part.at[col_y * levels + z, low], first.at[k, 1, 1], 3, k, dev_y),
+        ]
+
+    def stage_two(k, ones):
+        z = flip(level, k)
+        ones[0].wait_recv()
+        add(fold.at[k, 0], part.at[col_y * levels + z, top], first.at[k, 0, 0])
+        a = go(fold.at[k, 0], second.at[k, 0], 4, k, dev_y)
+        ones[1].wait_recv()
+        add(fold.at[k, 1], part.at[col_x * levels + z, low], first.at[k, 1, 0])
+        b = go(fold.at[k, 1], second.at[k, 1], 5, k, dev_x)
+        return [a, b]
+
+    def stage_three(k, ones, twos):
+        z = flip(level, k)
+        for copy in ones[2:] + twos:
+            copy.wait_recv()
+        for h, piece in enumerate((top, low)):
+            level_sum[k, piece] = (
+                part[col * levels + z, piece].astype(F32)
+                + first[k, h, 1].astype(F32)
+                + second[k, h].astype(F32)
+            ).astype(BF16)
+        if k:
+            return go(level_sum.at[k], third.at[k], 6, k, (col * 2 + core, flip(level, k)))
+
+    order = list(range(levels - 1, -1, -1))
+    ones, twos, threes = {}, {}, {}
+    ones[order[0]] = stage_one(order[0])
+    for n, k in enumerate(order):
+        if n + 1 < levels:
+            ones[order[n + 1]] = stage_one(order[n + 1])
+        twos[k] = stage_two(k, ones[k])
+        if n:
+            p = order[n - 1]
+            threes[p] = stage_three(p, ones[p], twos[p])
+    k = order[-1]
+    stage_three(k, ones[k], twos[k])
+    for m in range(1, levels):
+        threes[m].wait_recv()
+    total = level_sum[0].astype(F32)
+    for m in range(1, levels):
+        total = total + third[m].astype(F32)
+    out[...] = total.astype(BF16)
+    for copy in started:
+        copy.wait_send()
+
+
+def on_layers(levels, tokens, expert_ids, route_weights, w_gate, w_up, w_down):
+    tok_rows, width = tokens.shape
+    top_count = expert_ids.shape[1]
+    device_count = lax.axis_size("side") * levels
+    capacity = 2 * tok_rows * top_count // device_count
+    chips = device_count // 2
+    core = lax.axis_index("side") % 2
+    experts = jnp.arange(device_count, dtype=jnp.int32)
+    weight = jnp.sum(
+        jnp.where(expert_ids[:, None, :] == experts[None, :, None], route_weights[:, None, :], 0.0),
+        axis=2,
+    ).T
+    mine = weight.reshape(chips // levels, 2, levels, tok_rows).transpose(0, 2, 1, 3)
+    mine = mine.reshape(chips, 2, tok_rows)
+    mine = jnp.where(core == 1, mine[:, ::-1], mine)
+    mine = jnp.pad(mine, ((0, 0), (0, 6), (0, 0)))
+    anywhere = pl.BlockSpec(memory_space=pl.ANY)
+    dma = pltpu.SemaphoreType.DMA
+    shape = jax.ShapeDtypeStruct
+    every, shares, wg2, wu2, wd2 = pl.pallas_call(
+        functools.partial(gather_kernel, levels),
+        out_shape=[
+            shape((chips, tok_rows, width), BF16),
+            shape(mine.shape, F32),
+            shape(w_gate.shape, BF16),
+            shape(w_up.shape, BF16),
+            shape(w_down.shape, BF16),
+        ],
+        in_specs=[anywhere] * 5,
+        out_specs=[anywhere] * 5,
+        scratch_shapes=[
+            dma((7, levels)),
+            dma((7, levels)),
+            dma((chips - 1,)),
+            dma((chips - 1,)),
+            dma((3,)),
+            dma((3,)),
+            dma((2,)),
+        ],
+        compiler_params=pltpu.CompilerParams(collective_id=0, has_side_effects=True),
+        name="spread",
+    )(tokens, mine, w_gate, w_up, w_down)
+
+    weights = shares[:, :2]
+    chosen = weights > 0.0
+    before = jnp.triu(jnp.ones((tok_rows, tok_rows), BF16), 1)
+    slot = jnp.dot(chosen.astype(BF16).reshape(chips * 2, tok_rows), before, preferred_element_type=F32)
+    slot = slot.reshape(chips, 2, tok_rows).astype(jnp.int32)
+    table = (
+        slot[:, :, None, :] == jnp.arange(capacity, dtype=jnp.int32)[None, None, :, None]
+    ) & chosen[:, :, None, :]
+    pick = table.astype(BF16)
+    outputs = []
+    for i, (wg, wu, wd) in enumerate(((w_gate, w_up, w_down), (wg2, wu2, wd2))):
+        rows = jnp.einsum("bst,btd->bsd", pick[:, i], every, preferred_element_type=F32).astype(BF16)
+        rows = rows.reshape(chips * capacity, width)
+        gate = jnp.dot(rows, wg[0], preferred_element_type=F32)
+        upper = jnp.dot(rows, wu[0], preferred_element_type=F32)
+        hidden = (jax.nn.silu(gate) * upper).astype(BF16)
+        outputs.append(
+            jnp.dot(hidden, wd[0], preferred_element_type=F32)
+            .astype(BF16)
+            .reshape(chips, capacity, width)
+        )
+    back = jnp.where(table, weights[:, :, None, :], 0.0).astype(BF16)
+    back = back.reshape(chips, 2 * capacity, tok_rows)
+    part = jnp.einsum(
+        "bst,bsd->btd", back, jnp.concatenate(outputs, axis=1), preferred_element_type=F32
+    ).astype(BF16)
+
+    half = tok_rows // 2
+    vmem = pl.BlockSpec(memory_space=pltpu.VMEM)
+    return pl.pallas_call(
+        functools.partial(return_kernel, levels),
+        out_shape=shape((tok_rows, width), BF16),
+        in_specs=[vmem],
+        out_specs=vmem,
+        scratch_shapes=[
+            pltpu.VMEM((levels, 2, 2, half, width), BF16),
+            pltpu.VMEM((levels, 2, half, width), BF16),
+            pltpu.VMEM((levels, tok_rows, width), BF16),
+            pltpu.VMEM((levels, 2, half, width), BF16),
+            pltpu.VMEM((levels, tok_rows, width), BF16),
+            dma((7, levels)),
+            dma((7, levels)),
+        ],
+        compiler_params=pltpu.CompilerParams(
+            collective_id=1, has_side_effects=True, vmem_limit_bytes=56 * 2**20
+        ),
+        name="collect",
+    )(part)
 
 
 def expert_ffn(rows, gate_proj, up_proj, down_proj):
@@ -54,15 +334,28 @@
     return mixed.astype(jnp.bfloat16)
 
 
+def layered(mesh, tokens):
+    side, levels = mesh.shape["side"], mesh.shape["lane"]
+    layer_bytes = tokens.shape[0] // 2 * tokens.shape[1] * tokens.dtype.itemsize
+    return side == 2**3 and levels & (levels - 1) == 0 and 3 * layer_bytes < 32 * 2**20
+
+
 def solution(mesh):
     placed = (
-        P(("side", "lane"), None),
-        P(("side", "lane"), None),
-        P(("side", "lane"), None),
-        P(("side", "lane"), None, None),
-        P(("side", "lane"), None, None),
-        P(("side", "lane"), None, None),
-    )
-    return jax.shard_map(
-        on_device, mesh=mesh, in_specs=placed, out_specs=P(("side", "lane"), None), check_vma=False
-    )
+        P(AXES, None),
+        P(AXES, None),
+        P(AXES, None),
+        P(AXES, None, None),
+        P(AXES, None, None),
+        P(AXES, None, None),
+    )
+
+    def run(tokens, *rest):
+        body = on_device
+        if layered(mesh, tokens):
+            body = functools.partial(on_layers, mesh.shape["lane"])
+        return jax.shard_map(
+            body, mesh=mesh, in_specs=placed, out_specs=P(AXES, None), check_vma=False
+        )(tokens, *rest)
+
+    return run

time: 453 us -> 240 us (0.53)
  blocking collectives: 189 us -> 0 us
  waiting for transfers between devices: 181 us -> 0 us
  Pallas kernels: 0 us -> 175 us
  matrix products: 36.6 us -> 56.4 us
  local copies, waits for them, and re-layouts: 19.5 us -> 4.58 us
  other arithmetic: 17.3 us -> 2.91 us
  starting transfers between devices: 4.68 us -> 0 us
    all_to_all x1 -> x0, blocking collectives: 189 us -> none  [on_device(): lax.all_to_all(outgoing, ('side', 'lane'), split_axis=0, concat_axis=0, t...]
    all_to_all x1 -> x0, waiting for transfers between devices: 181 us -> none  [on_device(): lax.all_to_all(jnp.stack(results, axis=1).reshape(device_count * local_co...]
    pallas_call x0 -> x2, Pallas kernels: none -> 175 us  [the longest x1 91.2 us: on_layers(): pl.pallas_call(functools.partial(return_kernel, levels), out_shape=shape(...]
    dot_general x4 -> x8, matrix products: 36.6 us -> 56.4 us  [the longest x2 26.6 us: on_layers(): jnp.dot(hidden, wd[0], preferred_element_type=F32).astype(BF16)]
    gather x1 -> x0, local copies, waits for them, and re-layouts: 13.3 us -> none  [on_device(): picked = flat_back[position]]
    another operation x3 -> x0, other arithmetic: 9.15 us -> none
    reduce_or x1 -> x0, other arithmetic: 7.41 us -> none  [on_device(): jnp.any(buffer_rows[:, None, None] == position[None, :, :], axis=2)]
    all_to_all x1 -> x0, starting transfers between devices: 4.68 us -> none  [on_device(): lax.all_to_all(jnp.stack(results, axis=1).reshape(device_count * local_co...]
  transfers between devices with their start and end apart: 1 -> 0, of which waited for: 1 -> 0; matrix products, arithmetic and copies ran while one was open for 0% -> 0% of each run, Pallas kernels for 0% -> 0%
where the time goes in v2:
time: 240 us; the launch traced here: 239 us
  Pallas kernels  175 us (73%)
  matrix products  56.4 us (24%)
  local copies, waits for them, and re-layouts  4.58 us (2%)
  other arithmetic  2.91 us (1%)
    pallas_call x1, Pallas kernels, on_layers(): pl.pallas_call(functools.partial(return_kernel, levels), out_shape=shape(...  91.2 us
    pallas_call x1, Pallas kernels, on_layers(): pl.pallas_call(functools.partial(gather_kernel, levels), out_shape=[shape...  84.3 us
    dot_general x2, matrix products, on_layers(): jnp.dot(hidden, wd[0], preferred_element_type=F32).astype(BF16)  26.6 us
    dot_general x2, matrix products, on_layers(): upper = jnp.dot(rows, wu[0], preferred_element_type=F32)  12.4 us
    dot_general x1, matrix products, on_layers(): jnp.einsum('bst,bsd->btd', back, jnp.concatenate(outputs, axis=1), prefer...  9.07 us
    dot_general x2, matrix products, on_layers(): jnp.einsum('bst,btd->bsd', pick[:, i], every, preferred_element_type=F32)  8.23 us

profile of v2, /device:TPU:0, one launch (start us, length us, event | category | flops | bytes accessed | tf_op | source)
XLA Modules:
  0.0 239.4 jit_solution(14295082484252208401)
XLA Ops:
  0.0 0.1 eq.49
  0.1 0.7 select_reduce_fusion
  0.9 0.6 pad.4.mine
  1.6 84.3 %spread.1 = (bf16[16,128,2048]{2,1,0:T(8,128)(2,1)}, f32[16,8,128]{2,1,0:T(8,128)}, bf16[1,2048,768]{2,1,0:T(8,128)(2,1)}, bf16[1,2048,768]{2,1,0:T(8,128)(2,1)}, bf16[1,768,2048]{2,1,0:T(8,128)(2,1)}) custom-call(bf16[128,2048]{1,0:T(8,128)(2,1)} %tokens.1, f32[16,8,128]{2,1,0:T(8,128)} %pad.4.mine, bf16[1,2048,768]{2,1,0:T(8,128)(2,1)} %wg.1, ...), custom_call_target="tpu_custom_call" | custom-call | tf_op jit(solution)/shard_map/spread/pallas_call | solution.py:213
  85.9 0.9 broadcast_compare_fusion
  86.7 0.8 slice.9
  87.6 0.1 convolution_convert_fusion.4
  87.7 0.2 fusion.22
  88.0 0.0 slice-start
  88.0 1.1 fusion.21
  89.1 0.0 slice-start.1
  89.1 5.0 %convolution_convert_fusion.1 = bf16[16,64,2048]{2,1,0:T(8,128)(2,1)S(1)} fusion(bf16[16,128,2048]{2,1,0:T(8,128)(2,1)} %get-tuple-element.11, pred[16,2,64,128]{3,2,0,1:T(32,128)(4,1)S(1)} %fusion.22), kind=kOutput, calls=%fused_computation.6 | convolution fusion | flops 538968064 | bytes 12713984 | tf_op jit(solution)/shard_map/bst,btd->bsd/dot_general | solution.py:248
  94.1 0.0 slice-done
  94.1 0.2 slice-done.1
  94.2 0.0 copy-start
  94.2 0.0 copy-start.3
  94.2 3.2 %convolution_convert_fusion.3 = bf16[16,64,2048]{2,1,0:T(8,128)(2,1)} fusion(bf16[16,128,2048]{2,1,0:T(8,128)(2,1)S(1)} %bitcast.67, pred[16,2,64,128]{3,2,0,1:T(32,128)(4,1)S(1)} %fusion.22), kind=kOutput, calls=%fused_computation.8 | convolution fusion | flops 538968064 | bytes 12713984 | tf_op jit(solution)/shard_map/bst,btd->bsd/dot_general | solution.py:248
  97.5 0.6 copy-done
  98.0 0.3 copy-done.3
  98.4 5.1 %fusion.8 = f32[1024,768]{1,0:T(8,128)} fusion(bf16[1024,2048]{1,0:T(8,128)(2,1)S(1)} %bitcast.70, bf16[1,2048,768]{2,1,0:T(8,128)(2,1)S(1)} %copy-done.3), kind=kOutput, calls=%fused_computation.10 | convolution fusion | flops 3221225472 | bytes 10485760 | tf_op jit(solution)/shard_map/dot_general | solution.py:251
  103.4 0.0 copy-start.1
  103.4 13.4 %convolution_convert_fusion = bf16[1024,2048]{1,0:T(8,128)(2,1)} fusion(bf16[1,768,2048]{2,1,0:T(8,128)(2,1)} %get-tuple-element.14, f32[1024,768]{1,0:T(8,128)} %fusion.8, bf16[1024,2048]{1,0:T(8,128)(2,1)} %bitcast.71, bf16[1,2048,768]{2,1,0:T(8,128)(2,1)} %get-tuple-element.12), kind=kOutput, calls=%fused_computation.5 | convolution fusion | flops 6449266688 | bytes 17825792 | tf_op jit(solution)/shard_map/dot_general | solution.py:254
  116.8 0.0 copy-done.1
  116.8 7.3 %fusion.13 = f32[1024,768]{1,0:T(8,128)} fusion(bf16[1024,2048]{1,0:T(8,128)(2,1)} %bitcast.68, bf16[1,2048,768]{2,1,0:T(8,128)(2,1)S(1)} %copy-done.1), kind=kOutput, calls=%fused_computation.15 | convolution fusion | flops 3221225472 | bytes 10485760 | tf_op jit(solution)/shard_map/dot_general | solution.py:251
  124.1 0.0 copy-start.2
  124.1 13.2 %convolution_convert_fusion.2 = bf16[1024,2048]{1,0:T(8,128)(2,1)} fusion(bf16[1,768,2048]{2,1,0:T(8,128)(2,1)} %wd.1, f32[1024,768]{1,0:T(8,128)} %fusion.13, bf16[1024,2048]{1,0:T(8,128)(2,1)} %bitcast.69, bf16[1,2048,768]{2,1,0:T(8,128)(2,1)} %wg.1), kind=kOutput, calls=%fused_computation.7 | convolution fusion | flops 6449266688 | bytes 17825792 | tf_op jit(solution)/shard_map/dot_general | solution.py:254
  137.3 0.0 copy-done.2
  137.3 9.1 %fusion.4.part = bf16[16,128,2048]{2,1,0:T(8,128)(2,1)} fusion(bf16[16,128,128]{2,1,0:T(8,128)(2,1)S(1)} %copy-done.2, bf16[16,64,2048]{2,1,0:T(8,128)(2,1)} %bitcast.72, bf16[16,64,2048]{2,1,0:T(8,128)(2,1)} %bitcast.73), kind=kOutput, calls=%fused_computation.4 | convolution fusion | flops 1094713344 | bytes 17301504 | tf_op jit(solution)/shard_map/bst,bsd->btd/dot_general | solution.py:260
  146.4 91.2 %collect.1 = bf16[128,2048]{1,0:T(8,128)(2,1)} custom-call(bf16[16,128,2048]{2,1,0:T(8,128)(2,1)} %fusion.4.part), custom_call_target="tpu_custom_call" | custom-call | tf_op jit(solution)/shard_map/collect/pallas_call | solution.py:266
  237.6 1.9 copy.42
  (7 shorter events, 0.1 us)
Async XLA Ops:
  88.0 6.1 %slice-start = ((s8[8388608]{0:T(1024)(128)(4,1)}), s8[4194304]{0:T(1024)(128)(4,1)S(1)}, s32[]{:S(2)}) async-start(s8[8388608]{0:T(1024)(128)(4,1)} %bitcast.66), calls=%async_computation | async-start | bytes 8388608
  89.1 5.2 %slice-start.1 = ((s8[8388608]{0:T(1024)(128)(4,1)}), s8[4194304]{0:T(1024)(128)(4,1)S(1)}, s32[]{:S(2)}) async-start(s8[8388608]{0:T(1024)(128)(4,1)} %bitcast.66), calls=%async_computation.1 | async-start | bytes 8388608
  94.2 3.8 %copy-start = (bf16[16,64,2048]{2,1,0:T(8,128)(2,1)}, bf16[16,64,2048]{2,1,0:T(8,128)(2,1)S(1)}, u32[]{:S(2)}) copy-start(bf16[16,64,2048]{2,1,0:T(8,128)(2,1)S(1)} %convolution_convert_fusion.1) | copy-start | bytes 12582916
  94.2 4.1 %copy-start.3 = (bf16[1,2048,768]{2,1,0:T(8,128)(2,1)S(1)}, bf16[1,2048,768]{2,1,0:T(8,128)(2,1)}, u32[]{:S(2)}) copy-start(bf16[1,2048,768]{2,1,0:T(8,128)(2,1)} %get-tuple-element.13) | copy-start | bytes 9437188
  103.4 13.4 %copy-start.1 = (bf16[1,2048,768]{2,1,0:T(8,128)(2,1)S(1)}, bf16[1,2048,768]{2,1,0:T(8,128)(2,1)}, u32[]{:S(2)}) copy-start(bf16[1,2048,768]{2,1,0:T(8,128)(2,1)} %wu.1) | copy-start | bytes 9437188
  124.1 13.2 %copy-start.2 = (bf16[16,128,128]{2,1,0:T(8,128)(2,1)S(1)}, bf16[16,128,128]{2,1,0:T(8,128)(2,1)}, u32[]{:S(2)}) copy-start(bf16[16,128,128]{2,1,0:T(8,128)(2,1)} %fusion.21) | copy-start | bytes 1572868

commit v3 on v2

--- a/solution.py
+++ b/solution.py
@@ -111,7 +111,17 @@
         copy.wait()
 
 
-def return_kernel(levels, part, out, first, second, third, fold, level_sum, send, recv):
+def return_kernel(
+    levels, every, pick, back, wga, wua, wda, wgb, wub, wdb, out, wgs, wus, wds, xs, ys, part, first,
+    second, third, fold, level_sum, send, recv, fetch
+):
+    loads = [
+        pltpu.make_async_copy(src.at[0], dst.at[e], fetch.at[i, e])
+        for i, (dst, pair) in enumerate(((wgs, (wga, wgb)), (wus, (wua, wub)), (wds, (wda, wdb))))
+        for e, src in enumerate(pair)
+    ]
+    for copy in loads:
+        copy.start()
     col, core, level = place(levels)
     rows = out.shape[0]
     half = rows // 2
@@ -137,6 +147,32 @@
     def add(dst, one, two):
         dst[...] = (one[...].astype(F32) + two[...].astype(F32)).astype(BF16)
 
+    columns = every.shape[0] // levels
+    slots = pick.shape[1] // 2
+
+    def compute(k):
+        z = flip(level, k)
+        for j in range(columns):
+            b = j * levels + z
+            rows_b = jnp.dot(pick[b], every[b], preferred_element_type=F32).astype(BF16)
+            for e in range(2):
+                xs[e, pl.ds(j * slots, slots)] = rows_b[e * slots : (e + 1) * slots]
+
+        def expert(e, carry):
+            x = xs[e]
+            gate = jnp.dot(x, wgs[e], preferred_element_type=F32)
+            upper = jnp.dot(x, wus[e], preferred_element_type=F32)
+            hidden = (gate / (1.0 + jnp.exp(-gate)) * upper).astype(BF16)
+            ys[e] = jnp.dot(hidden, wds[e], preferred_element_type=F32).astype(BF16)
+            return carry
+
+        lax.fori_loop(0, 2, expert, 0)
+        for j in range(columns):
+            b = j * levels + z
+            mix = back[b]
+            y = jnp.concatenate([ys[e, pl.ds(j * slots, slots)] for e in range(2)], axis=0)
+            part[b] = jnp.dot(mix, y, preferred_element_type=F32).astype(BF16)
+
     def stage_one(k):
         z = flip(level, k)
         return [
@@ -171,16 +207,18 @@
 
     order = list(range(levels - 1, -1, -1))
     ones, twos, threes = {}, {}, {}
-    ones[order[0]] = stage_one(order[0])
-    for n, k in enumerate(order):
-        if n + 1 < levels:
-            ones[order[n + 1]] = stage_one(order[n + 1])
-        twos[k] = stage_two(k, ones[k])
-        if n:
+    for copy in loads:
+        copy.wait()
+    for n in range(levels + 2):
+        if n < levels:
+            compute(order[n])
+            ones[order[n]] = stage_one(order[n])
+        if 1 <= n <= levels:
             p = order[n - 1]
+            twos[p] = stage_two(p, ones[p])
+        if n >= 2:
+            p = order[n - 2]
             threes[p] = stage_three(p, ones[p], twos[p])
-    k = order[-1]
-    stage_three(k, ones[k], twos[k])
     for m in range(1, levels):
         threes[m].wait_recv()
     total = level_sum[0].astype(F32)
@@ -243,32 +281,23 @@
         slot[:, :, None, :] == jnp.arange(capacity, dtype=jnp.int32)[None, None, :, None]
     ) & chosen[:, :, None, :]
     pick = table.astype(BF16)
-    outputs = []
-    for i, (wg, wu, wd) in enumerate(((w_gate, w_up, w_down), (wg2, wu2, wd2))):
-        rows = jnp.einsum("bst,btd->bsd", pick[:, i], every, preferred_element_type=F32).astype(BF16)
-        rows = rows.reshape(chips * capacity, width)
-        gate = jnp.dot(rows, wg[0], preferred_element_type=F32)
-        upper = jnp.dot(rows, wu[0], preferred_element_type=F32)
-        hidden = (jax.nn.silu(gate) * upper).astype(BF16)
-        outputs.append(
-            jnp.dot(hidden, wd[0], preferred_element_type=F32)
-            .astype(BF16)
-            .reshape(chips, capacity, width)
-        )
     back = jnp.where(table, weights[:, :, None, :], 0.0).astype(BF16)
-    back = back.reshape(chips, 2 * capacity, tok_rows)
-    part = jnp.einsum(
-        "bst,bsd->btd", back, jnp.concatenate(outputs, axis=1), preferred_element_type=F32
-    ).astype(BF16)
-
+    back = back.reshape(chips, 2 * capacity, tok_rows).transpose(0, 2, 1)
+    pick = pick.reshape(chips, 2 * capacity, tok_rows)
     half = tok_rows // 2
     vmem = pl.BlockSpec(memory_space=pltpu.VMEM)
     return pl.pallas_call(
         functools.partial(return_kernel, levels),
         out_shape=shape((tok_rows, width), BF16),
-        in_specs=[vmem],
+        in_specs=[vmem] * 3 + [anywhere] * 6,
         out_specs=vmem,
         scratch_shapes=[
+            pltpu.VMEM((2,) + w_gate.shape[1:], BF16),
+            pltpu.VMEM((2,) + w_up.shape[1:], BF16),
+            pltpu.VMEM((2,) + w_down.shape[1:], BF16),
+            pltpu.VMEM((2, chips // levels * capacity, width), BF16),
+            pltpu.VMEM((2, chips // levels * capacity, width), BF16),
+            pltpu.VMEM((chips, tok_rows, width), BF16),
             pltpu.VMEM((levels, 2, 2, half, width), BF16),
             pltpu.VMEM((levels, 2, half, width), BF16),
             pltpu.VMEM((levels, tok_rows, width), BF16),
@@ -276,12 +305,13 @@
             pltpu.VMEM((levels, tok_rows, width), BF16),
             dma((7, levels)),
             dma((7, levels)),
+            dma((3, 2)),
         ],
         compiler_params=pltpu.CompilerParams(
-            collective_id=1, has_side_effects=True, vmem_limit_bytes=56 * 2**20
+            collective_id=1, has_side_effects=True, vmem_limit_bytes=60 * 2**20
         ),
         name="collect",
-    )(part)
+    )(every, pick, back, w_gate, w_up, w_down, wg2, wu2, wd2)
 
 
 def expert_ffn(rows, gate_proj, up_proj, down_proj):

time: 240 us -> 190 us (0.79)
  matrix products: 56.4 us -> 0.13 us
  Pallas kernels: 175 us -> 181 us
    dot_general x7 -> x0, matrix products: 56.3 us -> none  [the longest x2 26.6 us: on_layers(): jnp.dot(hidden, wd[0], preferred_element_type=F32).astype(BF16)]
    pallas_call x1, Pallas kernels: 91.2 us -> 96.5 us  [on_layers(): pl.pallas_call(functools.partial(return_kernel, levels), out_shape=shape(...]
where the time goes in v3:
time: 190 us
  Pallas kernels  181 us (95%)
  local copies, waits for them, and re-layouts  5.82 us (3%)
  other arithmetic  2.89 us (2%)
    pallas_call x1, Pallas kernels, on_layers(): pl.pallas_call(functools.partial(return_kernel, levels), out_shape=shape(...  96.5 us
    pallas_call x1, Pallas kernels, on_layers(): pl.pallas_call(functools.partial(gather_kernel, levels), out_shape=[shape...  84.3 us

profile of v3, /device:TPU:0, one launch (start us, length us, event | category | flops | bytes accessed | tf_op | source)
XLA Modules:
  0.0 189.8 jit_solution(15552887209450626975)
XLA Ops:
  0.0 0.7 select_reduce_fusion
  0.8 0.6 pad.4.mine
  1.5 84.3 %spread.1 = (bf16[16,128,2048]{2,1,0:T(8,128)(2,1)}, f32[16,8,128]{2,1,0:T(8,128)}, bf16[1,2048,768]{2,1,0:T(8,128)(2,1)}, bf16[1,2048,768]{2,1,0:T(8,128)(2,1)}, bf16[1,768,2048]{2,1,0:T(8,128)(2,1)}) custom-call(bf16[128,2048]{1,0:T(8,128)(2,1)} %tokens.1, f32[16,8,128]{2,1,0:T(8,128)} %pad.4.mine, bf16[1,2048,768]{2,1,0:T(8,128)(2,1)} %wga.1, ...), custom_call_target="tpu_custom_call" | custom-call | tf_op jit(solution)/shard_map/spread/pallas_call | solution.py:251
  85.8 0.9 broadcast_compare_fusion
  86.7 0.1 convolution_convert_fusion
  86.8 0.1 eq.43
  86.9 0.3 copy.26
  87.2 0.8 slice.3
  88.1 0.1 broadcast_in_dim.44
  88.1 0.3 copy.28
  88.4 0.1 and.19
  88.5 0.4 copy.27
  89.0 0.1 eq.46
  89.1 1.1 fusion
  90.2 0.1 convert_element_type.15
  90.3 1.0 copy.29.pick
  91.4 96.5 %collect.1 = bf16[128,2048]{1,0:T(8,128)(2,1)} custom-call(bf16[16,128,2048]{2,1,0:T(8,128)(2,1)} %get-tuple-element.10.every, bf16[16,128,128]{2,1,0:T(8,128)(2,1)} %copy.29.pick, bf16[16,128,128]{2,1,0:T(8,128)(2,1)} %get-tuple-element.15.back, bf16[1,2048,768]{2,1,0:T(8,128)(2,1)} %wga.1, bf16[1,2048,768]{2,1,0:T(8,128)(2,1)} %wua.1, ...), custom_call_target="tpu_custom_call" | custom-call | tf_op jit(solution)/shard_map/collect/pallas_call | solution.py:289
  187.9 1.9 copy.33
  (5 shorter events, 0.1 us)
